TPU v7x, 256 devices: a whole 4x4x8 slice. The times are simulated.
256 devices in a mesh: grp: 8 (over x, core), mem: 32 (over z, y).
Axes of the slice: x: 4, y: 4, z: 8, core: 2. Of those that a mesh axis runs over, the one named last changes fastest.
Arguments:
- slab: float32 [2048, 16384], P('mem', 'grp'), may hold values from 0 to 32, as said below
- tiles: float32 [8192, 16384], P('grp', 'mem'), may hold values from 0 to 1.05, as said below
- slot_rows: int32 [16, 32], P('grp'), may hold values from -1 to 3, as said below
Outputs:
- clustered: float32 [2048, 16384], P('grp', 'mem')
Inputs may be any that keep to these rules, and one draw needn't show every extreme that they name: For each group g and block column m, the used slots h (slot_rows[g * 2 + h, m] >= 0) come first and name distinct block rows of the group; unused slots hold -1. Each block column has at least one used slot in every group, and in every draw some group and block column has all 2 slots used. Entries are nonnegative, positive in the tiles of used slots, and zero in the tiles of unused slots. `slab`: entries are positive.
All inputs are finite; a program needn't handle non-finite values.
Results may differ from a plain program's by a relative error of at most 0.0003.
Values sent between devices are 32-bit elements; how exact they have to be, the bound alone decides.
A program may use at most 64 MiB of HBM per device.

v0:
```python
import jax
import jax.numpy as jnp
from jax import lax
from jax.sharding import PartitionSpec as P


def per_device(slab, tiles, slot_rows):
    tile_size = tiles.shape[1]
    slot_total = tiles.shape[0] // tile_size
    member = lax.axis_index("mem")
    own_rows = lax.dynamic_index_in_dim(slot_rows, member, axis=1, keepdims=False)
    used_slots = jnp.sum((own_rows >= 0).astype(jnp.int32))
    block_rows = jnp.maximum(own_rows, 0)
    tile_stack = tiles.reshape(slot_total, tile_size, tile_size)
    row_piece = lax.all_gather(slab, "mem", axis=0, tiled=True)

    def add_slot(slot_index, running):
        columns = lax.dynamic_slice_in_dim(
            row_piece, block_rows[slot_index] * tile_size, tile_size, 1
        )
        return running + jnp.dot(
            columns,
            tile_stack[slot_index],
            preferred_element_type=jnp.float32,
            precision=lax.Precision.HIGHEST,
        )

    partial_sums = lax.fori_loop(
        0, used_slots, add_slot, jnp.zeros((row_piece.shape[0], tile_size), jnp.float32)
    )
    window_rows = partial_sums.shape[0]
    expanded = lax.psum_scatter(partial_sums, "grp", scatter_dimension=0, tiled=True)
    inflated = expanded * expanded
    column_sums = lax.psum(jnp.sum(inflated, axis=0), "grp")
    column_means = column_sums / window_rows
    return inflated / column_means


def solution(mesh):
    return jax.shard_map(
        per_device,
        mesh=mesh,
        in_specs=(P("mem", "grp"), P("grp", "mem"), P("grp", None)),
        out_specs=P("grp", "mem"),
        check_vma=False,
    )
```

profile of v0, /device:TPU:1, one launch (start us, length us, event | category | flops | bytes accessed | tf_op | source)
XLA Modules:
  0.0 241.1 jit_solution(9636385513887879012)
XLA Ops:
  6.5 0.0 copy-start
  6.5 0.0 all-gather.2.cloned.1.call-start
  6.5 0.7 all-gather.2.cloned.1.call-update
  7.3 0.0 reduce-scatter.2.cloned.1.call-start
  7.3 1.4 maximum_reduce_fusion
  8.8 143.9 %all-gather.2.cloned.1.call-done = f32[2048,2048]{1,0:T(8,128)} async-done(((f32[64,2048]{1,0:T(8,128)}), f32[2048,2048]{1,0:T(8,128)}) %all-gather.2.cloned.1.call-update) | async-done | bytes 16777232 | tf_op jit(solution)/shard_map/all_gather | solution.py:15
  152.7 2.5 %broadcast_in_dim.4 = f32[2048,512]{1,0:T(8,128)} broadcast(f32[]{:T(128)} %constant.7.clone.1), dimensions={} | broadcast | bytes 4194308 | tf_op jit(solution)/shard_map/broadcast_in_dim | solution.py:29
  155.2 0.0 copy-done
  155.2 25.2 %while.10 = (s32[]{:T(128)}, f32[2048,512]{1,0:T(8,128)}, s32[]{:T(128)}, s32[2]{0:T(128)S(1)}, f32[2048,2048]{1,0:T(8,128)}, /*index=5*/f32[2,512,512]{2,1,0:T(...) while((s32[]{:T(128)}, f32[2048,512]{1,0:T(8,128)}, s32[]{:T(128)}, ...), condition=%wide.region_2.3_spmd, body=%wide.region_1.2_spmd.sunk | while | flops 6443499520 | bytes 13631705 | solution.py:28
  155.8 0.6 dynamic_slice.29
  157.0 10.4 %fusion.14 = f32[2048,512]{1,0:T(8,128)} fusion(f32[2048,512]{1,0:T(8,128)} %get-tuple-element.103, f32[2048,2048]{1,0:T(8,128)} %get-tuple-element.117, s32[]{:T(128)S(6)} %select_n.15, f32[2,512,512]{2,1,0:T(8,128)S(1)} %get-tuple-element.118, s32[]{:T(128)S(6)} %select_n.14), kind=kOutput, calls=%fused_computation.2.clone.1 | convolution fusion | flops 6443499520 | bytes 13631496 | tf_op jit(solution)/shard_map/while/body/dot_general | solution.py:21
  168.1 0.6 dynamic_slice.29
  169.3 10.4 %fusion.14 = f32[2048,512]{1,0:T(8,128)} fusion(f32[2048,512]{1,0:T(8,128)} %get-tuple-element.103, f32[2048,2048]{1,0:T(8,128)} %get-tuple-element.117, s32[]{:T(128)S(6)} %select_n.15, f32[2,512,512]{2,1,0:T(8,128)S(1)} %get-tuple-element.118, s32[]{:T(128)S(6)} %select_n.14), kind=kOutput, calls=%fused_computation.2.clone.1 | convolution fusion | flops 6443499520 | bytes 13631496 | tf_op jit(solution)/shard_map/while/body/dot_general | solution.py:21
  180.4 0.0 reduce-scatter.2.cloned.1.call-update
  180.4 35.7 %reduce-scatter.2.cloned.1.call-done = f32[256,512]{1,0:T(8,128)} async-done(((f32[2048,512]{1,0:T(8,128)}), f32[256,512]{1,0:T(8,128)}) %reduce-scatter.2.cloned.1.call-update) | async-done | bytes 524304 | tf_op jit(solution)/shard_map/reduce_scatter | solution.py:32
  216.1 1.1 multiply_reduce_fusion
  217.2 15.2 %psum.7 = f32[512]{0:T(512)S(1)} all-reduce(f32[512]{0:T(512)S(1)} %multiply_reduce_fusion), channel_id=1, replica_groups=mesh['grp'=8,'mem'=32] {'grp'}, use_global_device_ids=true, to_apply=%region_5.6 | all-reduce | flops 512 | bytes 4096 | tf_op jit(solution)/shard_map/psum | solution.py:34
  232.4 1.9 multiply_divide_fusion
  (1 shorter events, 0.0 us)
Async XLA Ops:
  6.5 148.6 %copy-start = (f32[1024,512]{1,0:T(8,128)S(1)}, f32[1024,512]{1,0:T(8,128)}, u32[]{:S(2)}) copy-start(f32[1024,512]{1,0:T(8,128)} %param.6) | copy-start | bytes 6291460
  6.5 146.2 %all-gather.2.cloned.1.call-start = ((), (), s32[]{:S(2)}) async-start(), calls=%async_computation.1 | async-start | bytes 17301504 | tf_op jit(solution)/shard_map/all_gather | solution.py:15
  7.3 208.8 %reduce-scatter.2.cloned.1.call-start = ((), (), s32[]{:S(2)}) async-start(), calls=%async_computation.2 | async-start | bytes 4718592 | tf_op jit(solution)/shard_map/reduce_scatter | solution.py:32
Sparse Core Ops, SparseCore 0:
  9.9 142.7 all-gather.1
  180.5 35.5 reduce-scatter.1
where the time goes:
time: 241 us
  waiting for transfers between devices  180 us (75%)
  matrix products  20.9 us (9%)
  blocking collectives  15.2 us (6%)
  between operations  13.4 us (6%)
  other arithmetic  4.47 us (2%)
  local copies, waits for them, and re-layouts  3.65 us (2%)
  loops' own time  3.12 us (1%)
    all_gather x1, waiting for transfers between devices, per_device(): row_piece = lax.all_gather(slab, 'mem', axis=0, tiled=True)  144 us
    reduce_scatter x1, waiting for transfers between devices, per_device(): lax.psum_scatter(partial_sums, 'grp', scatter_dimension=0, tiled=True)  35.7 us
    dot_general x2, matrix products, add_slot(): jnp.dot(columns, tile_stack[slot_index], preferred_element_type=jnp.float...  20.9 us
    psum x1, blocking collectives, per_device(): column_sums = lax.psum(jnp.sum(inflated, axis=0), 'grp')  15.2 us
  transfers between devices with their start and end apart: 2, of which 2 were waited for; matrix products, arithmetic and copies ran while one was open for 1% of the time, Pallas kernels for 0%

commit v1 on v0

--- a/solution.py
+++ b/solution.py
@@ -31,7 +31,7 @@
     window_rows = partial_sums.shape[0]
     expanded = lax.psum_scatter(partial_sums, "grp", scatter_dimension=0, tiled=True)
     inflated = expanded * expanded
-    column_sums = lax.psum(jnp.sum(inflated, axis=0), "grp")
+    column_sums = jnp.sum(lax.all_gather(jnp.sum(inflated, axis=0), "grp"), axis=0)
     column_means = column_sums / window_rows
     return inflated / column_means
 

time: 241 us -> 241 us (level)
    psum x1 -> x0, blocking collectives: 15.2 us -> none  [per_device(): column_sums = lax.psum(jnp.sum(inflated, axis=0), 'grp')]
    all_gather x0 -> x1, blocking collectives: none -> 14.5 us  [per_device(): lax.all_gather(jnp.sum(inflated, axis=0), 'grp')]
where the time goes in v1:
time: 241 us
  waiting for transfers between devices  180 us (75%)
  matrix products  20.9 us (9%)
  blocking collectives  14.5 us (6%)
  between operations  13.4 us (6%)
  other arithmetic  4.5 us (2%)
  local copies, waits for them, and re-layouts  3.65 us (2%)
  loops' own time  3.12 us (1%)
    all_gather x1, waiting for transfers between devices, per_device(): row_piece = lax.all_gather(slab, 'mem', axis=0, tiled=True)  144 us
    reduce_scatter x1, waiting for transfers between devices, per_device(): lax.psum_scatter(partial_sums, 'grp', scatter_dimension=0, tiled=True)  35.7 us
    dot_general x2, matrix products, add_slot(): jnp.dot(columns, tile_stack[slot_index], preferred_element_type=jnp.float...  20.9 us
    all_gather x1, blocking collectives, per_device(): lax.all_gather(jnp.sum(inflated, axis=0), 'grp')  14.5 us
  transfers between devices with their start and end apart: 2, of which 2 were waited for; matrix products, arithmetic and copies ran while one was open for 1% of the time, Pallas kernels for 0%

profile of v1, /device:TPU:1, one launch (start us, length us, event | category | flops | bytes accessed | tf_op | source)
XLA Modules:
  0.0 240.5 jit_solution(8992051125408662957)
XLA Ops:
  6.5 0.0 copy-start
  6.5 0.0 all-gather.4.cloned.1.call-start
  6.5 0.7 all-gather.4.cloned.1.call-update
  7.3 0.0 reduce-scatter.2.cloned.1.call-start
  7.3 1.4 maximum_reduce_fusion
  8.8 143.9 %all-gather.4.cloned.1.call-done = f32[2048,2048]{1,0:T(8,128)} async-done(((f32[64,2048]{1,0:T(8,128)}), f32[2048,2048]{1,0:T(8,128)}) %all-gather.4.cloned.1.call-update) | async-done | bytes 16777232 | tf_op jit(solution)/shard_map/all_gather | solution.py:15
  152.7 2.5 %broadcast_in_dim.4 = f32[2048,512]{1,0:T(8,128)} broadcast(f32[]{:T(128)} %constant.7.clone.1), dimensions={} | broadcast | bytes 4194308 | tf_op jit(solution)/shard_map/broadcast_in_dim | solution.py:29
  155.2 0.0 copy-done
  155.2 25.2 %while.10 = (s32[]{:T(128)}, f32[2048,512]{1,0:T(8,128)}, s32[]{:T(128)}, s32[2]{0:T(128)S(1)}, f32[2048,2048]{1,0:T(8,128)}, /*index=5*/f32[2,512,512]{2,1,0:T(...) while((s32[]{:T(128)}, f32[2048,512]{1,0:T(8,128)}, s32[]{:T(128)}, ...), condition=%wide.region_2.3_spmd, body=%wide.region_1.2_spmd.sunk | while | flops 6443499520 | bytes 13631705 | solution.py:28
  155.8 0.6 dynamic_slice.29
  157.0 10.4 %fusion.14 = f32[2048,512]{1,0:T(8,128)} fusion(f32[2048,512]{1,0:T(8,128)} %get-tuple-element.103, f32[2048,2048]{1,0:T(8,128)} %get-tuple-element.117, s32[]{:T(128)S(6)} %select_n.15, f32[2,512,512]{2,1,0:T(8,128)S(1)} %get-tuple-element.118, s32[]{:T(128)S(6)} %select_n.14), kind=kOutput, calls=%fused_computation.2.clone.1 | convolution fusion | flops 6443499520 | bytes 13631496 | tf_op jit(solution)/shard_map/while/body/dot_general | solution.py:21
  168.1 0.6 dynamic_slice.29
  169.3 10.4 %fusion.14 = f32[2048,512]{1,0:T(8,128)} fusion(f32[2048,512]{1,0:T(8,128)} %get-tuple-element.103, f32[2048,2048]{1,0:T(8,128)} %get-tuple-element.117, s32[]{:T(128)S(6)} %select_n.15, f32[2,512,512]{2,1,0:T(8,128)S(1)} %get-tuple-element.118, s32[]{:T(128)S(6)} %select_n.14), kind=kOutput, calls=%fused_computation.2.clone.1 | convolution fusion | flops 6443499520 | bytes 13631496 | tf_op jit(solution)/shard_map/while/body/dot_general | solution.py:21
  180.4 0.0 reduce-scatter.2.cloned.1.call-update
  180.4 35.7 %reduce-scatter.2.cloned.1.call-done = f32[256,512]{1,0:T(8,128)} async-done(((f32[2048,512]{1,0:T(8,128)}), f32[256,512]{1,0:T(8,128)}) %reduce-scatter.2.cloned.1.call-update) | async-done | bytes 524304 | tf_op jit(solution)/shard_map/reduce_scatter | solution.py:32
  216.1 1.1 multiply_reduce_fusion
  217.2 14.5 %all-gather.1 = f32[8,1,512]{2,1,0:T(1,128)S(1)} all-gather(f32[1,1,512]{2,1,0:T(1,128)S(1)} %bitcast.11), channel_id=2, replica_groups=mesh['grp'=8,'mem'=32] {'grp'}, dimensions={0}, use_global_device_ids=true | all-gather | bytes 18432 | tf_op jit(solution)/shard_map/all_gather | solution.py:34
  231.8 1.9 multiply_divide_fusion
  (2 shorter events, 0.0 us)
Async XLA Ops:
  6.5 148.6 %copy-start = (f32[1024,512]{1,0:T(8,128)S(1)}, f32[1024,512]{1,0:T(8,128)}, u32[]{:S(2)}) copy-start(f32[1024,512]{1,0:T(8,128)} %param.6) | copy-start | bytes 6291460
  6.5 146.2 %all-gather.4.cloned.1.call-start = ((), (), s32[]{:S(2)}) async-start(), calls=%async_computation.1 | async-start | bytes 17301504 | tf_op jit(solution)/shard_map/all_gather | solution.py:15
  7.3 208.8 %reduce-scatter.2.cloned.1.call-start = ((), (), s32[]{:S(2)}) async-start(), calls=%async_computation.2 | async-start | bytes 4718592 | tf_op jit(solution)/shard_map/reduce_scatter | solution.py:32
Sparse Core Ops, SparseCore 0:
  9.9 142.7 all-gather.3
  180.5 35.5 reduce-scatter.1

commit v2 on v0

--- a/solution.py
+++ b/solution.py
@@ -12,7 +12,9 @@
     used_slots = jnp.sum((own_rows >= 0).astype(jnp.int32))
     block_rows = jnp.maximum(own_rows, 0)
     tile_stack = tiles.reshape(slot_total, tile_size, tile_size)
-    row_piece = lax.all_gather(slab, "mem", axis=0, tiled=True)
+    row_piece = jnp.concatenate(
+        lax.all_to_all(jnp.stack([slab] * lax.axis_size("mem")), "mem", 0, 0), axis=0
+    )
 
     def add_slot(slot_index, running):
         columns = lax.dynamic_slice_in_dim(

time: 241 us -> 522 us (2.17)
  waiting for transfers between devices: 180 us -> 440 us
  starting transfers between devices: 0.04 us -> 12.3 us
  local copies, waits for them, and re-layouts: 3.65 us -> 12.6 us
    all_to_all x0 -> x1, waiting for transfers between devices: none -> 369 us  [per_device(): lax.all_to_all(jnp.stack([slab] * lax.axis_size('mem')), 'mem', 0, 0)]
    all_gather x1 -> x0, waiting for transfers between devices: 144 us -> none  [per_device(): row_piece = lax.all_gather(slab, 'mem', axis=0, tiled=True)]
    reduce_scatter x1, waiting for transfers between devices: 35.7 us -> 71 us  [per_device(): lax.psum_scatter(partial_sums, 'grp', scatter_dimension=0, tiled=True)]
    all_to_all x0 -> x1, starting transfers between devices: none -> 12.3 us  [per_device(): lax.all_to_all(jnp.stack([slab] * lax.axis_size('mem')), 'mem', 0, 0)]
    another operation x0 -> x1, local copies, waits for them, and re-layouts: none -> 8.9 us  [per_device(): jnp.stack([slab] * lax.axis_size('mem'))]
  transfers between devices with their start and end apart: 2 -> 2, of which waited for: 2 -> 2; matrix products, arithmetic and copies ran while one was open for 1% -> 0% of each run, Pallas kernels for 0% -> 0%
where the time goes in v2:
time: 522 us
  waiting for transfers between devices  440 us (84%)
  matrix products  20.9 us (4%)
  blocking collectives  15.2 us (3%)
  between operations  13.4 us (3%)
  local copies, waits for them, and re-layouts  12.6 us (2%)
  starting transfers between devices  12.3 us (2%)
    all_to_all x1, waiting for transfers between devices, per_device(): lax.all_to_all(jnp.stack([slab] * lax.axis_size('mem')), 'mem', 0, 0)  369 us
    reduce_scatter x1, waiting for transfers between devices, per_device(): lax.psum_scatter(partial_sums, 'grp', scatter_dimension=0, tiled=True)  71 us
    dot_general x2, matrix products, add_slot(): jnp.dot(columns, tile_stack[slot_index], preferred_element_type=jnp.float...  20.9 us
    psum x1, blocking collectives, per_device(): column_sums = lax.psum(jnp.sum(inflated, axis=0), 'grp')  15.2 us
    all_to_all x1, starting transfers between devices, per_device(): lax.all_to_all(jnp.stack([slab] * lax.axis_size('mem')), 'mem', 0, 0)  12.3 us
  transfers between devices with their start and end apart: 2, of which 2 were waited for; matrix products, arithmetic and copies ran while one was open for 0% of the time, Pallas kernels for 0%

profile of v2, /device:TPU:1, one launch (start us, length us, event | category | flops | bytes accessed | tf_op | source)
XLA Modules:
  0.0 522.0 jit_solution(12755862472772971109)
XLA Ops:
  6.5 8.9 %stack.2 = f32[32,64,2048]{2,1,0:T(8,128)} broadcast(f32[64,2048]{1,0:T(8,128)} %param.5), dimensions={1,2} | broadcast | bytes 17301504 | tf_op jit(solution)/shard_map/stack | solution.py:16
  15.4 0.0 copy-start.1
  15.4 12.3 %all-to-all-start = ((f32[32,64,2048]{2,1,0:T(8,128)}), f32[32,64,2048]{2,1,0:T(8,128)}, u32[]{:S(2)}, u32[]{:S(2)}) async-start(f32[32,64,2048]{2,1,0:T(8,128)} %stack.2), calls=%async_computation | async-start | bytes 33554432 | tf_op jit(solution)/shard_map/all_to_all | solution.py:16
  27.7 0.0 copy-start
  27.7 0.0 reduce-scatter.2.cloned.1.call-start
  27.8 0.0 copy-done.1
  27.8 0.8 maximum_reduce_fusion
  28.6 369.4 %all-to-all-done = f32[32,64,2048]{2,1,0:T(8,128)} async-done(((f32[32,64,2048]{2,1,0:T(8,128)}), f32[32,64,2048]{2,1,0:T(8,128)}, u32[]{:S(2)}, u32[]{:S(2)}) %all-to-all-start) | async-done | bytes 16777248 | tf_op jit(solution)/shard_map/all_to_all | solution.py:16
  398.0 2.5 broadcast_in_dim.4
  400.5 0.0 copy-done
  400.5 25.4 %while.10 = (s32[]{:T(128)}, f32[2048,512]{1,0:T(8,128)}, s32[]{:T(128)}, s32[2]{0:T(128)S(1)}, f32[2048,2048]{1,0:T(8,128)}, /*index=5*/f32[2,512,512]{2,1,0:T(...) while((s32[]{:T(128)}, f32[2048,512]{1,0:T(8,128)}, s32[]{:T(128)}, ...), condition=%wide.region_2.3_spmd, body=%wide.region_1.2_spmd.sunk | while | flops 6443499520 | bytes 13631697 | solution.py:30
  401.1 0.6 dynamic_slice.29
  402.4 10.4 %fusion.14 = f32[2048,512]{1,0:T(8,128)} fusion(f32[2048,512]{1,0:T(8,128)} %get-tuple-element.103, f32[2048,2048]{1,0:T(8,128)} %get-tuple-element.117, s32[]{:T(128)S(6)} %select_n.15, f32[2,512,512]{2,1,0:T(8,128)S(1)} %get-tuple-element.118, s32[]{:T(128)S(6)} %select_n.14), kind=kOutput, calls=%fused_computation.2.clone.1 | convolution fusion | flops 6443499520 | bytes 13631496 | tf_op jit(solution)/shard_map/while/body/dot_general | solution.py:23
  413.5 0.6 dynamic_slice.29
  414.8 10.4 %fusion.14 = f32[2048,512]{1,0:T(8,128)} fusion(f32[2048,512]{1,0:T(8,128)} %get-tuple-element.103, f32[2048,2048]{1,0:T(8,128)} %get-tuple-element.117, s32[]{:T(128)S(6)} %select_n.15, f32[2,512,512]{2,1,0:T(8,128)S(1)} %get-tuple-element.118, s32[]{:T(128)S(6)} %select_n.14), kind=kOutput, calls=%fused_computation.2.clone.1 | convolution fusion | flops 6443499520 | bytes 13631496 | tf_op jit(solution)/shard_map/while/body/dot_general | solution.py:23
  425.9 0.0 reduce-scatter.2.cloned.1.call-update
  425.9 71.0 %reduce-scatter.2.cloned.1.call-done = f32[256,512]{1,0:T(8,128)} async-done(((f32[2048,512]{1,0:T(8,128)}), f32[256,512]{1,0:T(8,128)}) %reduce-scatter.2.cloned.1.call-update) | async-done | bytes 524304 | tf_op jit(solution)/shard_map/reduce_scatter | solution.py:34
  496.9 1.1 multiply_reduce_fusion
  498.1 15.2 %psum.7 = f32[512]{0:T(512)S(1)} all-reduce(f32[512]{0:T(512)S(1)} %multiply_reduce_fusion), channel_id=1, replica_groups=mesh['grp'=8,'mem'=32] {'grp'}, use_global_device_ids=true, to_apply=%region_5.6 | all-reduce | flops 512 | bytes 4096 | tf_op jit(solution)/shard_map/psum | solution.py:36
  513.2 1.9 multiply_divide_fusion
  (1 shorter events, 0.0 us)
Async XLA Ops:
  15.4 12.4 %copy-start.1 = (s32[2,32]{1,0:T(2,128)S(1)}, s32[2,32]{1,0:T(2,128)}, u32[]{:S(2)}) copy-start(s32[2,32]{1,0:T(2,128)} %param.7) | copy-start | bytes 772
  15.4 382.6 %all-to-all-start = ((f32[32,64,2048]{2,1,0:T(8,128)}), f32[32,64,2048]{2,1,0:T(8,128)}, u32[]{:S(2)}, u32[]{:S(2)}) async-start(f32[32,64,2048]{2,1,0:T(8,128)} %stack.2), calls=%async_computation | async-start | bytes 33554432 | tf_op jit(solution)/shard_map/all_to_all | solution.py:16
  27.7 372.7 %copy-start = (f32[1024,512]{1,0:T(8,128)S(1)}, f32[1024,512]{1,0:T(8,128)}, u32[]{:S(2)}) copy-start(f32[1024,512]{1,0:T(8,128)} %param.6) | copy-start | bytes 6291460
  27.7 469.2 %reduce-scatter.2.cloned.1.call-start = ((), (), s32[]{:S(2)}) async-start(), calls=%async_computation.2 | async-start | bytes 4718592 | tf_op jit(solution)/shard_map/reduce_scatter | solution.py:34
Sparse Core Ops, SparseCore 0:
  426.0 70.8 reduce-scatter.1
